TPU v7x, 16 devices: a 4x2x1 block of a 4x4x8 slice. The times are simulated.
16 devices in a mesh: dp: 2 (over y, z), tp: 8 (over x, core).
Axes of the slice: x: 4, y: 2, z: 1, core: 2. Of those that a mesh axis runs over, the one named last changes fastest.
The devices are a block of a 4x4x8 slice.
Arguments:
- x: bfloat16 [4096, 2048], P('dp'), parts along dimension 0
- w_gate: bfloat16 [2048, 8192], P(None, 'tp')
- w_up: bfloat16 [2048, 8192], P(None, 'tp')
- w_down: bfloat16 [8192, 2048], P('tp')
Outputs:
- output: bfloat16 [4096, 2048], P('dp'), parts along dimension 0
There are 2 independent parts. A program takes and returns all parts, laid end to end along the dimension named above; an argument that names none is the same for every part.
All inputs are finite; a program needn't handle non-finite values.
Results may differ from a plain program's by a relative error of at most 0.016.
Values are sent between devices in bfloat16 or wider.
A program may use at most 768 MiB of HBM per device.

v0:
```python
import jax
import jax.numpy as jnp
from jax import lax
from jax.sharding import PartitionSpec as P


def solution(mesh):
    def step(x, w_gate, w_up, w_down):
        gate = jnp.dot(x, w_gate, preferred_element_type=jnp.float32)
        up = jnp.dot(x, w_up, preferred_element_type=jnp.float32)
        hidden = (jax.nn.silu(gate) * up).astype(jnp.bfloat16)
        term = jnp.dot(hidden, w_down, preferred_element_type=jnp.float32).astype(jnp.bfloat16)
        return lax.psum(term, "tp")

    return jax.shard_map(
        step,
        mesh=mesh,
        in_specs=(P("dp", None), P(None, "tp"), P(None, "tp"), P("tp", None)),
        out_specs=P("dp", None),
        check_vma=False,
    )
```

profile of v0, /device:TPU:113, one launch (start us, length us, event | category | flops | bytes accessed | tf_op | source)
XLA Modules:
  0.0 160.9 jit_solution(6648705555156849355)
XLA Ops:
  6.5 0.0 all-reduce.2.cloned.1.call-start
  6.6 14.5 %fusion.2 = f32[2048,1024]{1,0:T(8,128)} fusion(bf16[2048,2048]{1,0:T(8,128)(2,1)} %param.4, bf16[2048,1024]{1,0:T(8,128)(2,1)} %param.5), kind=kOutput, calls=%fused_computation.4 | convolution fusion | flops 8589934592 | bytes 20971520 | tf_op jit(solution)/shard_map/dot_general | solution.py:9
  21.0 26.0 %convolution_convert_fusion = bf16[2048,2048]{1,0:T(8,128)(2,1)} fusion(bf16[1024,2048]{1,0:T(8,128)(2,1)} %param.7, f32[2048,1024]{1,0:T(8,128)} %fusion.2, bf16[2048,2048]{1,0:T(8,128)(2,1)} %param.4, bf16[2048,1024]{1,0:T(8,128)(2,1)} %param.6), kind=kOutput, calls=%fused_computation.1 | convolution fusion | flops 17196646400 | bytes 33554432 | tf_op jit(solution)/shard_map/dot_general | solution.py:12
  47.0 0.1 all-reduce.2.cloned.1.call-update
  47.0 98.6 %all-reduce.2.cloned.1.call-done = bf16[2048,2048]{1,0:T(8,128)(2,1)} async-done(((bf16[2048,2048]{1,0:T(8,128)(2,1)}), bf16[2048,2048]{1,0:T(8,128)(2,1)}) %all-reduce.2.cloned.1.call-update) | async-done | bytes 8388624 | tf_op jit(solution)/shard_map/psum | solution.py:13
  145.6 8.4 %copy.6 = bf16[2048,2048]{1,0:T(8,128)(2,1)} copy(bf16[2048,2048]{1,0:T(8,128)(2,1)} %all-reduce.2.cloned.1.call-done) | data formatting | bytes 16777216
Async XLA Ops:
  6.5 139.1 %all-reduce.2.cloned.1.call-start = ((), (), s32[]{:S(2)}) async-start(), calls=%async_computation | async-start | bytes 16777216 | tf_op jit(solution)/shard_map/psum | solution.py:13
Sparse Core Ops, SparseCore 0:
  47.1 98.4 all-reduce.1
where the time goes:
time: 161 us
  waiting for transfers between devices  98.6 us (61%)
  matrix products  40.4 us (25%)
  between operations  13.4 us (8%)
  local copies, waits for them, and re-layouts  8.44 us (5%)
    psum x1, waiting for transfers between devices, step(): return lax.psum(term, 'tp')  98.6 us
    dot_general x1, matrix products, step(): jnp.dot(hidden, w_down, preferred_element_type=jnp.float32)  26 us
    dot_general x1, matrix products, step(): gate = jnp.dot(x, w_gate, preferred_element_type=jnp.float32)  14.5 us
    unnamed x1, local copies, waits for them, and re-layouts  8.44 us
  transfers between devices with their start and end apart: 1, of which 1 were waited for; matrix products, arithmetic and copies ran while one was open for 0% of the time, Pallas kernels for 0%

commit v1 on v0

v1 whole, which is shorter than its diff:
```python
import functools

import jax
import jax.numpy as jnp
from jax import lax
from jax.experimental import pallas as pl
from jax.experimental.pallas import tpu as pltpu
from jax.sharding import PartitionSpec as P

MESH = pl.DeviceIdType.MESH
F32, BF16 = jnp.float32, jnp.bfloat16
CORES = 2
SUBS = 2
FIRST_TILES, GATE_TILES = 4, 2
FIRST_CUTS, CUTS = 4, 2
LAST_CUTS = 4
GROUP = 16


def tile(i, width):
    start = i * width
    return pl.ds(start if isinstance(start, int) else pl.multiple_of(start, width), width)


def mlp_kernel(n, x, wg, wu, wd, y, xs, wgv, wuv, wdv, hid, own, give, got, part, run, *sems):
    (x_sem, g_sem, u_sem, d_sem, give_sem, got_sem, part_sem, run_sem, gs_sem, gr_sem, os_sem, or_sem) = sems
    rows, depth = x.shape
    units = wg.shape[1]
    chunk = rows // n
    half = chunk // CORES
    p = half // SUBS
    blocks = n * SUBS

    me = lax.axis_index("tp")
    chip, core = me // CORES, me % CORES
    way = 1 - 2 * core
    peer = me + way
    ahead = ((chip + way + n) % n) * CORES + core
    behind = ((chip - way + n) % n) * CORES + core

    def my_rows(s, j):
        start = ((chip - way * (1 + s) + n) % n) * chunk + core * half + j * p
        return pl.multiple_of(start, p)

    def peer_rows(s, j):
        start = ((chip + way * (1 + s) + n) % n) * chunk + (1 - core) * half + j * p
        return pl.multiple_of(start, p)

    def remote(src, dst, ssem, rsem, to):
        return pltpu.make_async_remote_copy(
            src_ref=src, dst_ref=dst, send_sem=ssem, recv_sem=rsem, device_id={"tp": to}, device_id_type=MESH
        )

    barrier = pltpu.get_barrier_semaphore()
    for other in (peer, ahead, behind):
        pl.semaphore_signal(barrier, inc=1, device_id={"tp": other}, device_id_type=MESH)

    def x_copies(b):
        s, j = b // SUBS, b % SUBS
        return (
            pltpu.make_async_copy(x.at[pl.ds(my_rows(s, j), p)], xs.at[b, pl.ds(0, p)], x_sem.at[b, 0]),
            pltpu.make_async_copy(x.at[pl.ds(peer_rows(s, j), p)], xs.at[b, pl.ds(p, p)], x_sem.at[b, 1]),
        )

    def gate_copies(i):
        c = tile(i, units // FIRST_TILES)
        return (
            pltpu.make_async_copy(wg.at[:, c], wgv.at[:, c], g_sem.at[i]),
            pltpu.make_async_copy(wu.at[:, c], wuv.at[:, c], u_sem.at[i]),
        )

    def down_copy(i):
        c = tile(i, depth // FIRST_CUTS)
        return pltpu.make_async_copy(wd.at[:, c], wdv.at[:, c], d_sem.at[i])

    for c in x_copies(0):
        c.start()
    for i in range(FIRST_TILES):
        for c in gate_copies(i):
            c.start()
    for i in range(FIRST_CUTS):
        down_copy(i).start()

    def hidden(b, i, tiles):
        c = tile(i, units // tiles)
        g = jnp.dot(xs[b], wgv[:, c], preferred_element_type=F32)
        u = jnp.dot(xs[b], wuv[:, c], preferred_element_type=F32)
        hid[:, c] = (jax.nn.silu(g) * u).astype(BF16)

    def give_copy(b, q, cuts):
        c = tile(q, depth // cuts)
        return remote(give.at[b, :, c], got.at[b, :, c], give_sem.at[b, q], got_sem.at[b, q], peer)

    def down(b, q, cuts):
        c = tile(q, depth // cuts)
        term = jnp.dot(hid[...], wdv[:, c], preferred_element_type=F32)
        own[b, :, c] = term[:p]
        give[b, :, c] = term[p:].astype(BF16)
        give_copy(b, q, cuts).start()

    def run_copy(b, q, cuts):
        c = tile(q, depth // cuts)
        return remote(part.at[b, :, c], run.at[b, :, c], part_sem.at[b, q], run_sem.at[b, q], ahead)

    def ring_copy(k, j, q, cuts):
        at = pl.ds(my_rows(k - 1, j) + q * (p // cuts), p // cuts)
        return remote(y.at[at], y.at[at], gs_sem.at[k * SUBS + j, q], gr_sem.at[k * SUBS + j, q], ahead)

    def over_copy(k, j, q, cuts):
        at = pl.ds(my_rows(k - 1, j) + q * (p // cuts), p // cuts)
        return remote(y.at[at], y.at[at], os_sem.at[k * SUBS + j, q], or_sem.at[k * SUBS + j, q], peer)

    def over_arrival(k, j, q, cuts):
        at = pl.ds(peer_rows(k - 1, j) + q * (p // cuts), p // cuts)
        return remote(y.at[at], y.at[at], os_sem.at[k * SUBS + j, q], or_sem.at[k * SUBS + j, q], peer)

    def ring_arrival(k, j, q, cuts):
        at = pl.ds(my_rows(k, j) + q * (p // cuts), p // cuts)
        return remote(y.at[at], y.at[at], gs_sem.at[k * SUBS + j, q], gr_sem.at[k * SUBS + j, q], ahead)

    def cuts_of(b):
        return FIRST_CUTS if b == 0 else CUTS

    def hop_cuts(k):
        return LAST_CUTS if k == n - 2 else 1

    def over_cuts(k):
        return LAST_CUTS if k == n - 1 else 1

    def add(b, c, before, dst, base):
        def body(i, _):
            at = tile(i, GROUP)
            total = own[b, at, c] + got[b, at, c].astype(F32)
            if before:
                total = total + run[b - SUBS, at, c].astype(F32)
            if dst is y:
                y[pl.ds(pl.multiple_of(base + i * GROUP, GROUP), GROUP), c] = total.astype(BF16)
            else:
                part[b, at, c] = total.astype(BF16)
            return 0

        lax.fori_loop(0, p // GROUP, body, 0)

    for b in range(blocks):
        s, j = b // SUBS, b % SUBS
        tiles, cuts = (FIRST_TILES if b == 0 else GATE_TILES), cuts_of(b)
        for c in x_copies(b):
            c.wait()

        def gate_up(i, _):
            if b == 0:
                for c in gate_copies(i):
                    c.wait()
            hidden(b, i, tiles)
            return 0

        lax.fori_loop(0, tiles, gate_up, 0)
        if b == 0:
            for later in range(1, blocks):
                for c in x_copies(later):
                    c.start()
            pl.semaphore_wait(barrier, 3)

        def out(q, _):
            if b == 0:
                down_copy(q).wait()
            down(b, q, cuts)
            return 0

        lax.fori_loop(0, cuts, out, 0)

        if s > 0:
            for q in range(cuts_of(b - SUBS)):
                run_copy(b - SUBS, q, cuts_of(b - SUBS)).wait_recv()
        for q in range(cuts):
            give_copy(b, q, cuts).wait_recv()
            c = tile(q, depth // cuts)
            if s < n - 1:
                add(b, c, s > 0, part, 0)
                run_copy(b, q, cuts).start()
            else:
                add(b, c, True, y, my_rows(s, j))
        if s == n - 1:
            for q in range(hop_cuts(0)):
                ring_copy(0, j, q, hop_cuts(0)).start()
            for q in range(over_cuts(0)):
                over_copy(0, j, q, over_cuts(0)).start()

    for k in range(n - 1):
        for j in range(SUBS):
            cuts = hop_cuts(k)
            for q in range(cuts):
                ring_arrival(k, j, q, cuts).wait_recv()
                if over_cuts(k + 1) == cuts:
                    over_copy(k + 1, j, q, cuts).start()
            if k + 1 < n - 1:
                for q in range(hop_cuts(k + 1)):
                    ring_copy(k + 1, j, q, hop_cuts(k + 1)).start()

    for b in range(blocks):
        for q in range(cuts_of(b)):
            give_copy(b, q, cuts_of(b)).wait_send()
            if b // SUBS < n - 1:
                run_copy(b, q, cuts_of(b)).wait_send()
    for k in range(n):
        for j in range(SUBS):
            if k < n - 1:
                for q in range(hop_cuts(k)):
                    ring_copy(k, j, q, hop_cuts(k)).wait_send()
            for q in range(over_cuts(k)):
                over_copy(k, j, q, over_cuts(k)).wait_send()
                over_arrival(k, j, q, over_cuts(k)).wait_recv()


def write_kernel(pieces, y, out, sem):
    r = y.shape[0] // pieces
    copies = [pltpu.make_async_copy(y.at[tile(i, r)], out.at[tile(i, r)], sem.at[i]) for i in range(pieces)]
    for c in copies:
        c.start()
    for c in copies:
        c.wait()


def solution(mesh):
    n = mesh.shape["tp"] // CORES

    def step(x, w_gate, w_up, w_down):
        rows, depth = x.shape
        units = w_gate.shape[1]
        p = rows // n // CORES // SUBS
        blocks = n * SUBS
        dma = pltpu.SemaphoreType.DMA
        most = max(FIRST_CUTS, CUTS)
        y = pl.pallas_call(
            functools.partial(mlp_kernel, n),
            out_shape=pltpu.VMEM((rows, depth), BF16),
            in_specs=[pl.BlockSpec(memory_space=pl.ANY)] * 4,
            out_specs=pl.BlockSpec(memory_space=pltpu.VMEM),
            scratch_shapes=[
                pltpu.VMEM((blocks, CORES * p, depth), BF16),
                pltpu.VMEM((depth, units), BF16),
                pltpu.VMEM((depth, units), BF16),
                pltpu.VMEM((units, depth), BF16),
                pltpu.VMEM((CORES * p, units), BF16),
                pltpu.VMEM((blocks, p, depth), F32),
                pltpu.VMEM((blocks, p, depth), BF16),
                pltpu.VMEM((blocks, p, depth), BF16),
                pltpu.VMEM((blocks - SUBS, p, depth), BF16),
                pltpu.VMEM((blocks - SUBS, p, depth), BF16),
                dma((blocks, CORES)),
                dma((FIRST_TILES,)),
                dma((FIRST_TILES,)),
                dma((FIRST_CUTS,)),
                dma((blocks, most)),
                dma((blocks, most)),
                dma((blocks - SUBS, most)),
                dma((blocks - SUBS, most)),
                dma((blocks - SUBS, LAST_CUTS)),
                dma((blocks - SUBS, LAST_CUTS)),
                dma((blocks, LAST_CUTS)),
                dma((blocks, LAST_CUTS)),
            ],
            compiler_params=pltpu.CompilerParams(
                collective_id=0, has_side_effects=True, vmem_limit_bytes=52 * 2**20
            ),
            cost_estimate=pl.CostEstimate(
                flops=6 * rows * depth * units, bytes_accessed=2 * rows * depth + 6 * depth * units, transcendentals=rows * units
            ),
        )(x, w_gate, w_up, w_down)
        pieces = 8
        return pl.pallas_call(
            functools.partial(write_kernel, pieces),
            out_shape=jax.ShapeDtypeStruct((rows, depth), BF16),
            in_specs=[pl.BlockSpec(memory_space=pltpu.VMEM)],
            out_specs=pl.BlockSpec(memory_space=pltpu.HBM),
            scratch_shapes=[dma((pieces,))],
            compiler_params=pltpu.CompilerParams(has_side_effects=True, vmem_limit_bytes=4 * 2**20),
        )(y)

    return jax.shard_map(
        step,
        mesh=mesh,
        in_specs=(P("dp", None), P(None, "tp"), P(None, "tp"), P("tp", None)),
        out_specs=P("dp", None),
        check_vma=False,
    )
```

time: 161 us -> 89.2 us (0.55)
  waiting for transfers between devices: 98.6 us -> 0 us
  Pallas kernels: 0 us -> 89.2 us
  matrix products: 40.4 us -> 0 us
  between operations: 13.4 us -> 0.01 us
  local copies, waits for them, and re-layouts: 8.44 us -> 0 us
    psum x1 -> x0, waiting for transfers between devices: 98.6 us -> none  [step(): return lax.psum(term, 'tp')]
    pallas_call x0 -> x2, Pallas kernels: none -> 89.2 us  [the longest x1 85.8 us: step(): pl.pallas_call(functools.partial(mlp_kernel, n), out_shape=pltpu.VMEM((ro...]
    dot_general x2 -> x0, matrix products: 40.4 us -> none  [the longest x1 26 us: step(): jnp.dot(hidden, w_down, preferred_element_type=jnp.float32)]
    unnamed x1 -> x0, local copies, waits for them, and re-layouts: 8.44 us -> none
  transfers between devices with their start and end apart: 1 -> 0, of which waited for: 1 -> 0; matrix products, arithmetic and copies ran while one was open for 0% -> 0% of each run, Pallas kernels for 0% -> 0%
where the time goes in v1:
time: 89.2 us
  Pallas kernels  89.2 us (100%)
    pallas_call x1, Pallas kernels, step(): pl.pallas_call(functools.partial(mlp_kernel, n), out_shape=pltpu.VMEM((ro...  85.8 us
    pallas_call x1, Pallas kernels, step(): pl.pallas_call(functools.partial(write_kernel, pieces), out_shape=jax.Sha...  3.37 us

profile of v1, /device:TPU:113, one launch (start us, length us, event | category | flops | bytes accessed | tf_op | source)
XLA Modules:
  0.0 89.2 jit_solution(9598833156100409771)
XLA Ops:
  0.0 85.8 %shard_map.46.y = bf16[2048,2048]{1,0:T(8,128)(2,1)S(1)} custom-call(bf16[2048,2048]{1,0:T(8,128)(2,1)} %x.1, bf16[2048,1024]{1,0:T(8,128)(2,1)} %wg.1, bf16[2048,1024]{1,0:T(8,128)(2,1)} %wu.1, bf16[1024,2048]{1,0:T(8,128)(2,1)} %wd.1), custom_call_target="tpu_custom_call" | custom-call | flops 25769803776 | bytes 20971520 | tf_op jit(solution)/shard_map/pallas_call | solution.py:234
  85.8 3.4 %shard_map.47 = bf16[2048,2048]{1,0:T(8,128)(2,1)} custom-call(bf16[2048,2048]{1,0:T(8,128)(2,1)S(1)} %shard_map.46.y), custom_call_target="tpu_custom_call" | custom-call | tf_op jit(solution)/shard_map/pallas_call | solution.py:271

commit v2 on v1

--- a/solution.py
+++ b/solution.py
@@ -23,7 +23,7 @@
 
 
 def mlp_kernel(n, x, wg, wu, wd, y, xs, wgv, wuv, wdv, hid, own, give, got, part, run, *sems):
-    (x_sem, g_sem, u_sem, d_sem, give_sem, got_sem, part_sem, run_sem, gs_sem, gr_sem, os_sem, or_sem) = sems
+    x_sem, g_sem, d_sem, give_sem, got_sem, part_sem, run_sem, ring_sem, ringed_sem, over_sem, overed_sem = sems
     rows, depth = x.shape
     units = wg.shape[1]
     chunk = rows // n
@@ -58,28 +58,27 @@
     def x_copies(b):
         s, j = b // SUBS, b % SUBS
         return (
-            pltpu.make_async_copy(x.at[pl.ds(my_rows(s, j), p)], xs.at[b, pl.ds(0, p)], x_sem.at[b, 0]),
-            pltpu.make_async_copy(x.at[pl.ds(peer_rows(s, j), p)], xs.at[b, pl.ds(p, p)], x_sem.at[b, 1]),
+            pltpu.make_async_copy(x.at[pl.ds(my_rows(s, j), p)], xs.at[b, pl.ds(0, p)], x_sem.at[b]),
+            pltpu.make_async_copy(x.at[pl.ds(peer_rows(s, j), p)], xs.at[b, pl.ds(p, p)], x_sem.at[b]),
         )
 
     def gate_copies(i):
         c = tile(i, units // FIRST_TILES)
         return (
             pltpu.make_async_copy(wg.at[:, c], wgv.at[:, c], g_sem.at[i]),
-            pltpu.make_async_copy(wu.at[:, c], wuv.at[:, c], u_sem.at[i]),
+            pltpu.make_async_copy(wu.at[:, c], wuv.at[:, c], g_sem.at[i]),
         )
 
     def down_copy(i):
         c = tile(i, depth // FIRST_CUTS)
         return pltpu.make_async_copy(wd.at[:, c], wdv.at[:, c], d_sem.at[i])
 
-    for c in x_copies(0):
-        c.start()
-    for i in range(FIRST_TILES):
-        for c in gate_copies(i):
-            c.start()
-    for i in range(FIRST_CUTS):
-        down_copy(i).start()
+    def start(*copies, later=1):
+        for c in copies:
+            c.start(priority=later)
+
+    start(*x_copies(0), *gate_copies(0), later=0)
+    start(*gate_copies(1))
 
     def hidden(b, i, tiles):
         c = tile(i, units // tiles)
@@ -87,9 +86,15 @@
         u = jnp.dot(xs[b], wuv[:, c], preferred_element_type=F32)
         hid[:, c] = (jax.nn.silu(g) * u).astype(BF16)
 
+    def got_at(b, q):
+        return q if b == 0 else FIRST_CUTS + q if b == 1 else FIRST_CUTS + CUTS + b - 2
+
     def give_copy(b, q, cuts):
         c = tile(q, depth // cuts)
-        return remote(give.at[b, :, c], got.at[b, :, c], give_sem.at[b, q], got_sem.at[b, q], peer)
+        return remote(give.at[b, :, c], got.at[b, :, c], give_sem, got_sem.at[got_at(b, q)], peer)
+
+    def gave(b):
+        return remote(give.at[b], got.at[b], give_sem, got_sem.at[got_at(b, 0)], peer)
 
     def down(b, q, cuts):
         c = tile(q, depth // cuts)
@@ -100,23 +105,18 @@
 
     def run_copy(b, q, cuts):
         c = tile(q, depth // cuts)
-        return remote(part.at[b, :, c], run.at[b, :, c], part_sem.at[b, q], run_sem.at[b, q], ahead)
+        return remote(part.at[b, :, c], run.at[b, :, c], part_sem, run_sem.at[b], ahead)
+
+    def ran(b):
+        return remote(part.at[b], run.at[b], part_sem, run_sem.at[b], ahead)
 
     def ring_copy(k, j, q, cuts):
         at = pl.ds(my_rows(k - 1, j) + q * (p // cuts), p // cuts)
-        return remote(y.at[at], y.at[at], gs_sem.at[k * SUBS + j, q], gr_sem.at[k * SUBS + j, q], ahead)
+        return remote(y.at[at], y.at[at], ring_sem, ringed_sem.at[k * SUBS + j * cuts + q], ahead)
 
     def over_copy(k, j, q, cuts):
         at = pl.ds(my_rows(k - 1, j) + q * (p // cuts), p // cuts)
-        return remote(y.at[at], y.at[at], os_sem.at[k * SUBS + j, q], or_sem.at[k * SUBS + j, q], peer)
-
-    def over_arrival(k, j, q, cuts):
-        at = pl.ds(peer_rows(k - 1, j) + q * (p // cuts), p // cuts)
-        return remote(y.at[at], y.at[at], os_sem.at[k * SUBS + j, q], or_sem.at[k * SUBS + j, q], peer)
-
-    def ring_arrival(k, j, q, cuts):
-        at = pl.ds(my_rows(k, j) + q * (p // cuts), p // cuts)
-        return remote(y.at[at], y.at[at], gs_sem.at[k * SUBS + j, q], gr_sem.at[k * SUBS + j, q], ahead)
+        return remote(y.at[at], y.at[at], over_sem, overed_sem, peer)
 
     def cuts_of(b):
         return FIRST_CUTS if b == 0 else CUTS
@@ -141,45 +141,74 @@
 
         lax.fori_loop(0, p // GROUP, body, 0)
 
-    for b in range(blocks):
-        s, j = b // SUBS, b % SUBS
-        tiles, cuts = (FIRST_TILES if b == 0 else GATE_TILES), cuts_of(b)
+    def finish(b, q):
+        s, j, cuts = b // SUBS, b % SUBS, cuts_of(b)
+        c = tile(q, depth // cuts)
+        if s < n - 1:
+            add(b, c, s > 0, part, 0)
+            run_copy(b, q, cuts).start()
+        else:
+            add(b, c, True, y, my_rows(s, j))
+
+    for c in x_copies(0):
+        c.wait()
+    for i in range(FIRST_TILES):
+        for c in gate_copies(i):
+            c.wait()
+        if i + 2 < FIRST_TILES:
+            start(*gate_copies(i + 2))
+        elif i + 2 == FIRST_TILES:
+            start(down_copy(0), down_copy(1))
+        else:
+            start(*[down_copy(q) for q in range(2, FIRST_CUTS)])
+        hidden(0, i, FIRST_TILES)
+    pl.semaphore_wait(barrier, 3)
+    for q in range(FIRST_CUTS):
+        down_copy(q).wait()
+        if q == FIRST_CUTS - 1:
+            start(*x_copies(1), *x_copies(2))
+            give_copy(0, 0, FIRST_CUTS).wait_recv()
+            finish(0, 0)
+        down(0, q, FIRST_CUTS)
+    def arrive(b):
         for c in x_copies(b):
             c.wait()
 
-        def gate_up(i, _):
-            if b == 0:
-                for c in gate_copies(i):
-                    c.wait()
-            hidden(b, i, tiles)
+    for q in range(1, FIRST_CUTS):
+        if q == FIRST_CUTS - 1:
+            arrive(1)
+            hidden(1, 0, GATE_TILES)
+        give_copy(0, q, FIRST_CUTS).wait_recv()
+        finish(0, q)
+    for b in range(3, blocks):
+        start(*x_copies(b))
+
+    for b in range(1, blocks):
+        s, j = b // SUBS, b % SUBS
+        for i in range(1, GATE_TILES):
+            hidden(b, i, GATE_TILES)
+
+        def out(q, _):
+            down(b, q, CUTS)
             return 0
 
-        lax.fori_loop(0, tiles, gate_up, 0)
-        if b == 0:
-            for later in range(1, blocks):
-                for c in x_copies(later):
-                    c.start()
-            pl.semaphore_wait(barrier, 3)
-
-        def out(q, _):
-            if b == 0:
-                down_copy(q).wait()
-            down(b, q, cuts)
-            return 0
-
-        lax.fori_loop(0, cuts, out, 0)
-
+        lax.fori_loop(0, CUTS, out, 0)
+        if b == 1:
+            for q in range(CUTS - 1):
+                give_copy(b, q, CUTS).wait_recv()
+                finish(b, q)
+        if b + 1 < blocks:
+            arrive(b + 1)
+            hidden(b + 1, 0, GATE_TILES)
+        if b == 1:
+            give_copy(b, CUTS - 1, CUTS).wait_recv()
+            finish(b, CUTS - 1)
+            continue
         if s > 0:
-            for q in range(cuts_of(b - SUBS)):
-                run_copy(b - SUBS, q, cuts_of(b - SUBS)).wait_recv()
-        for q in range(cuts):
-            give_copy(b, q, cuts).wait_recv()
-            c = tile(q, depth // cuts)
-            if s < n - 1:
-                add(b, c, s > 0, part, 0)
-                run_copy(b, q, cuts).start()
-            else:
-                add(b, c, True, y, my_rows(s, j))
+            ran(b - SUBS).wait_recv()
+        gave(b).wait_recv()
+        for q in range(CUTS):
+            finish(b, q)
         if s == n - 1:
             for q in range(hop_cuts(0)):
                 ring_copy(0, j, q, hop_cuts(0)).start()
@@ -190,26 +219,18 @@
         for j in range(SUBS):
             cuts = hop_cuts(k)
             for q in range(cuts):
-                ring_arrival(k, j, q, cuts).wait_recv()
+                ring_copy(k, j, q, cuts).wait_recv()
                 if over_cuts(k + 1) == cuts:
                     over_copy(k + 1, j, q, cuts).start()
             if k + 1 < n - 1:
                 for q in range(hop_cuts(k + 1)):
                     ring_copy(k + 1, j, q, hop_cuts(k + 1)).start()
 
-    for b in range(blocks):
-        for q in range(cuts_of(b)):
-            give_copy(b, q, cuts_of(b)).wait_send()
-            if b // SUBS < n - 1:
-                run_copy(b, q, cuts_of(b)).wait_send()
-    for k in range(n):
-        for j in range(SUBS):
-            if k < n - 1:
-                for q in range(hop_cuts(k)):
-                    ring_copy(k, j, q, hop_cuts(k)).wait_send()
-            for q in range(over_cuts(k)):
-                over_copy(k, j, q, over_cuts(k)).wait_send()
-                over_arrival(k, j, q, over_cuts(k)).wait_recv()
+    whole = y.at[pl.ds(0, rows // CORES)]
+    remote(give, got, give_sem, got_sem.at[0], peer).wait_send()
+    remote(part, run, part_sem, run_sem.at[0], ahead).wait_send()
+    remote(y.at[pl.ds(0, (n - 1) * half)], y.at[pl.ds(0, (n - 1) * half)], ring_sem, ringed_sem.at[0], ahead).wait_send()
+    remote(whole, whole, over_sem, overed_sem, peer).wait()
 
 
 def write_kernel(pieces, y, out, sem):
@@ -230,7 +251,6 @@
         p = rows // n // CORES // SUBS
         blocks = n * SUBS
         dma = pltpu.SemaphoreType.DMA
-        most = max(FIRST_CUTS, CUTS)
         y = pl.pallas_call(
             functools.partial(mlp_kernel, n),
             out_shape=pltpu.VMEM((rows, depth), BF16),
@@ -247,18 +267,17 @@
                 pltpu.VMEM((blocks, p, depth), BF16),
                 pltpu.VMEM((blocks - SUBS, p, depth), BF16),
                 pltpu.VMEM((blocks - SUBS, p, depth), BF16),
-                dma((blocks, CORES)),
-                dma((FIRST_TILES,)),
+                dma((blocks,)),
                 dma((FIRST_TILES,)),
                 dma((FIRST_CUTS,)),
-                dma((blocks, most)),
-                dma((blocks, most)),
-                dma((blocks - SUBS, most)),
-                dma((blocks - SUBS, most)),
-                dma((blocks - SUBS, LAST_CUTS)),
-                dma((blocks - SUBS, LAST_CUTS)),
-                dma((blocks, LAST_CUTS)),
-                dma((blocks, LAST_CUTS)),
+                dma,
+                dma((FIRST_CUTS + CUTS + blocks - 2,)),
+                dma,
+                dma((blocks - SUBS,)),
+                dma,
+                dma((blocks - SUBS * 2 + SUBS * LAST_CUTS,)),
+                dma,
+                dma,
             ],
             compiler_params=pltpu.CompilerParams(
                 collective_id=0, has_side_effects=True, vmem_limit_bytes=52 * 2**20

time: 89.2 us -> 85.2 us (0.955)
  Pallas kernels: 89.2 us -> 84.9 us
    pallas_call x1, Pallas kernels: 85.8 us -> 81.5 us  [step(): pl.pallas_call(functools.partial(mlp_kernel, n), out_shape=pltpu.VMEM((ro...]
where the time goes in v2:
time: 85.2 us; the launch traced here: 85.1 us
  Pallas kernels  84.9 us (100%)
    pallas_call x1, Pallas kernels, step(): pl.pallas_call(functools.partial(mlp_kernel, n), out_shape=pltpu.VMEM((ro...  81.5 us
    pallas_call x1, Pallas kernels, step(): pl.pallas_call(functools.partial(write_kernel, pieces), out_shape=jax.Sha...  3.37 us

profile of v2, /device:TPU:113, one launch (start us, length us, event | category | flops | bytes accessed | tf_op | source)
XLA Modules:
  0.0 85.1 jit_solution(7403738639642134884)
XLA Ops:
  0.0 81.5 %shard_map.46.y = bf16[2048,2048]{1,0:T(8,128)(2,1)S(1)} custom-call(bf16[2048,2048]{1,0:T(8,128)(2,1)} %x.1, bf16[2048,1024]{1,0:T(8,128)(2,1)} %wg.1, bf16[2048,1024]{1,0:T(8,128)(2,1)} %wu.1, bf16[1024,2048]{1,0:T(8,128)(2,1)} %wd.1), custom_call_target="tpu_custom_call" | custom-call | flops 25769803776 | bytes 20971520 | tf_op jit(solution)/shard_map/pallas_call | solution.py:254
  81.5 3.4 %shard_map.47 = bf16[2048,2048]{1,0:T(8,128)(2,1)} custom-call(bf16[2048,2048]{1,0:T(8,128)(2,1)S(1)} %shard_map.46.y), custom_call_target="tpu_custom_call" | custom-call | tf_op jit(solution)/shard_map/pallas_call | solution.py:290
